TPU v7x, 32 devices: a whole 2x2x4 slice. The times are simulated.
32 devices in a mesh: det: 8 (over z, y), row: 4 (over x, core).
Axes of the slice: x: 2, y: 2, z: 4, core: 2. Of those that a mesh axis runs over, the one named last changes fastest.
Arguments:
- science: float32 [8, 128, 768], P('det', 'row'), may hold values from -6 to 6
- template: float32 [8, 6, 128, 128], P('det', None, 'row'), may hold values from -6 to 6
- tile_source: int32 [8, 6], replicated, may hold values from 0 to 47, as said below
- offsets: int32 [2, 8, 6], P(None, 'det'), may hold values from 0 to 3
- shift_weights: float32 [2, 8, 6], P(None, 'det'), may hold values from 0 to 1
- valid_rows: int32 [8, 6], P('det'), may hold values from 32 to 128
- basis_kernels: float32 [27, 31, 31], replicated, may hold values from -0.1875 to 0.1875
- coefficients: float32 [8, 27], P('det'), may hold values from -1.25 to 1.25
- background: float32 [8], P('det'), may hold values from -4 to 4
Outputs:
- difference_tiles: float32 [8, 6, 128, 128], P('det', None, 'row')
Inputs may be any that keep to these rules, and one draw needn't show every extreme that they name: `tile_source`: entry [d, c] names slot s of sky patch p as p * 6 + s. Row d names the patches (d + j) mod 8 for j = 0 .. 3, in that order along the columns, each in one run of consecutive columns that names consecutive slots, 1 to 3 tiles long; one run of each row is exactly 3 long.
All inputs are finite; a program needn't handle non-finite values.
Results may differ from a plain program's by a relative error of at most 0.000062.
Values sent between devices are 32-bit elements; how exact they have to be, the bound alone decides.
No kernel may reach another device: no remote copies, remote signals or barrier semaphores. Data moves between devices by JAX's collectives and lax.ppermute only.
A program may use at most 64 MiB of HBM per device.

v0:
```python
import jax
import jax.numpy as jnp
from jax import lax
from jax.sharding import PartitionSpec as P

MAXOFF = 4
SPAN = 4


def shifted(value, axis, steps):
    count = lax.axis_size(axis)
    pairs = [(source, (source + steps) % count) for source in range(count)]
    return lax.ppermute(value, axis, pairs)


def with_halo(block, sides, width):
    for axis, dim in sides:
        count = lax.axis_size(axis)
        forward = [(i, i + 1) for i in range(count - 1)]
        backward = [(target, source) for source, target in forward]
        low = lax.ppermute(
            lax.slice_in_dim(block, block.shape[dim] - width, None, axis=dim), axis, forward
        )
        high = lax.ppermute(lax.slice_in_dim(block, 0, width, axis=dim), axis, backward)
        block = jnp.concatenate([low, block, high], axis=dim)
    return block


def run_ranks(row_sources, slot_count):
    owners = row_sources // slot_count
    order = jnp.arange(row_sources.shape[0], dtype=jnp.int32)
    same_owner = owners[:, None] == owners[None, :]
    earlier = order[None, :] < order[:, None]
    ranks = jnp.sum(jnp.logical_and(same_owner, earlier).astype(jnp.int32), axis=1)
    return (owners, ranks)


def body(
    science,
    template,
    tile_source,
    offsets,
    shift_weights,
    valid_rows,
    basis_kernels,
    coefficients,
    background,
):
    highest = lax.Precision.HIGHEST
    band_rows = science.shape[1]
    columns = science.shape[2]
    tile_size = template.shape[3]
    slot_count = template.shape[1]
    tile_count = columns // tile_size
    detectors = tile_source.shape[0]
    kernel_width = basis_kernels.shape[1]
    half_width = kernel_width // 2
    capacity = tile_count // 2
    det_index = lax.axis_index("det")
    row_index = lax.axis_index("row")
    row_devices = lax.axis_size("row")
    deep_width = half_width + MAXOFF
    rank_ids = jnp.arange(capacity, dtype=jnp.int32)
    slot_range = jnp.arange(slot_count, dtype=jnp.int32)

    def send_routing(reach):
        target = (det_index - reach) % detectors
        row_sources = lax.dynamic_index_in_dim(tile_source, target, 0, keepdims=False)
        owners, ranks = run_ranks(row_sources, slot_count)
        rank_hot = jnp.logical_and(
            ranks[:, None] == rank_ids[None, :], (owners == det_index)[:, None]
        ).astype(jnp.float32)
        slot_hot = ((row_sources % slot_count)[:, None] == slot_range[None, :]).astype(jnp.float32)
        return jnp.einsum("ck,cs->ks", rank_hot, slot_hot, precision=highest)

    routings = [send_routing(reach) for reach in range(SPAN)]
    own_sources = lax.dynamic_index_in_dim(tile_source, det_index, 0, keepdims=False)
    own_owners, own_ranks = run_ranks(own_sources, slot_count)
    own_reach = (own_owners - det_index) % detectors
    reach_hot = own_reach[:, None] == jnp.arange(SPAN, dtype=jnp.int32)[None, :]
    own_rank_hot = own_ranks[:, None] == rank_ids[None, :]
    picking = jnp.logical_and(reach_hot[:, :, None], own_rank_hot[:, None, :]).astype(jnp.float32)
    stored = template[0]
    outgoing = [
        jnp.einsum("ks,syi->kyi", routings[reach], stored, precision=highest)
        for reach in range(SPAN)
    ]
    received = [outgoing[0]]
    for reach in range(1, SPAN):
        received.append(shifted(outgoing[reach], "det", -reach))
    incoming = jnp.stack(received)
    arranged = jnp.einsum("cjk,jkyi->yci", picking, incoming, precision=highest)
    raw_band = arranged.reshape(arranged.shape[0], columns)
    row_shift = offsets[0, 0]
    column_shift = offsets[1, 0]
    row_weight = shift_weights[0, 0]
    column_weight = shift_weights[1, 0]
    pixel_ids = jnp.arange(tile_size, dtype=jnp.int32)
    first_index = jnp.minimum(pixel_ids[None, :] + column_shift[:, None], tile_size - 1)
    second_index = jnp.minimum(pixel_ids[None, :] + column_shift[:, None] + 1, tile_size - 1)
    first_select = (pixel_ids[None, :, None] == first_index[:, None, :]).astype(jnp.float32)
    second_select = (pixel_ids[None, :, None] == second_index[:, None, :]).astype(jnp.float32)
    shift_ids = jnp.arange(MAXOFF + 1, dtype=jnp.int32)
    row_coeffs = (1.0 - row_weight)[None, :] * (shift_ids[:, None] == row_shift[None, :]).astype(
        jnp.float32
    )
    row_coeffs = row_coeffs + row_weight[None, :] * (
        shift_ids[:, None] == row_shift[None, :] + 1
    ).astype(jnp.float32)
    column_coeffs = jnp.repeat(row_coeffs, tile_size, axis=1)
    extended = with_halo(raw_band, (("row", 0),), deep_width)
    blocks = extended.reshape(extended.shape[0], tile_count, tile_size)
    left_part = jnp.einsum("ycj,cji->yci", blocks, first_select, precision=highest)
    right_part = jnp.einsum("ycj,cji->yci", blocks, second_select, precision=highest)
    mixed = (1.0 - column_weight)[None, :, None] * left_part + column_weight[
        None, :, None
    ] * right_part
    across = mixed.reshape(extended.shape[0], columns)
    row_total = band_rows + 2 * half_width
    result = jnp.zeros((row_total, columns), jnp.float32)
    for shift_step in range(MAXOFF + 1):
        result = (
            result
            + column_coeffs[shift_step][None, :]
            * across[MAXOFF + shift_step : MAXOFF + shift_step + row_total]
        )
    warped_ext = result
    global_rows = (
        row_index * band_rows - half_width + jnp.arange(band_rows + 2 * half_width, dtype=jnp.int32)
    )
    inside = jnp.logical_and(global_rows >= 0, global_rows < row_devices * band_rows)
    warped_ext = jnp.where(inside[:, None], warped_ext, jnp.float32(0.0))
    kernel = jnp.einsum("k,kab->ab", coefficients[0], basis_kernels, precision=highest)
    tap_ids = jnp.arange(kernel_width, dtype=jnp.int32)
    lead_hot = (
        pixel_ids[:, None, None] - pixel_ids[None, :, None] == tap_ids[None, None, :]
    ).astype(jnp.float32)
    lead_bands = jnp.einsum("jib,ab->aji", lead_hot, kernel, precision=highest)
    trail_ids = jnp.arange(kernel_width - 1, dtype=jnp.int32)
    trail_hot = (
        tile_size + trail_ids[:, None, None] - pixel_ids[None, :, None] == tap_ids[None, None, :]
    ).astype(jnp.float32)
    trail_bands = jnp.einsum("jib,ab->aji", trail_hot, kernel, precision=highest)
    padded = jnp.pad(warped_ext, ((0, 0), (half_width, tile_size - half_width)))

    def kernel_row(tap_row, summed):
        rows_here = lax.dynamic_slice_in_dim(padded, tap_row, band_rows, 0)
        main_part = rows_here[:, :columns].reshape(band_rows, tile_count, tile_size)
        next_part = rows_here[:, tile_size:].reshape(band_rows, tile_count, tile_size)[
            :, :, : kernel_width - 1
        ]
        lead_now = lax.dynamic_index_in_dim(lead_bands, tap_row, 0, keepdims=False)
        trail_now = lax.dynamic_index_in_dim(trail_bands, tap_row, 0, keepdims=False)
        summed = summed + jnp.einsum("ycj,ji->yci", main_part, lead_now, precision=highest)
        return summed + jnp.einsum("ycj,ji->yci", next_part, trail_now, precision=highest)

    modelled = lax.fori_loop(
        0, kernel_width, kernel_row, jnp.zeros((band_rows, tile_count, tile_size), jnp.float32)
    )
    residual_image = science[0].reshape(band_rows, tile_count, tile_size) - modelled - background[0]
    band_global = row_index * band_rows + jnp.arange(band_rows, dtype=jnp.int32)
    usable = band_global[:, None] < valid_rows[0][None, :]
    residual_image = jnp.where(usable[:, :, None], residual_image, jnp.float32(0.0))
    returning = jnp.einsum("cjk,yci->jkyi", picking, residual_image, precision=highest)
    returned = [returning[0]]
    for reach in range(1, SPAN):
        returned.append(shifted(returning[reach], "det", reach))
    summed = jnp.zeros(stored.shape[:1] + (band_rows, tile_size), jnp.float32)
    tallies = jnp.zeros((slot_count,), jnp.float32)
    for reach in range(SPAN):
        summed = summed + jnp.einsum(
            "ks,kyi->syi", routings[reach], returned[reach], precision=highest
        )
        tallies = tallies + jnp.sum(routings[reach], axis=0)
    result = summed / jnp.maximum(tallies, 1.0)[:, None, None]
    return result[None]


def solution(mesh):
    in_specs = (
        P("det", "row", None),
        P("det", None, "row", None),
        P(),
        P(None, "det", None),
        P(None, "det", None),
        P("det", None),
        P(),
        P("det", None),
        P("det"),
    )
    out_specs = P("det", None, "row", None)
    return jax.shard_map(body, mesh=mesh, in_specs=in_specs, out_specs=out_specs, check_vma=False)
```

profile of v0, /device:TPU:1, one launch (start us, length us, event | category | flops | bytes accessed | tf_op | source)
XLA Modules:
  0.0 94.3 jit_solution(15203796628860832358)
XLA Ops:
  2.1 1.2 %fusion.29 = f32[3,32,128]{2,0,1:T(4,128)S(1)} fusion(f32[6,32,128]{2,1,0:T(8,128)} %bitcast.208, f32[3,6]{1,0:T(4,128)S(1)} %get-tuple-element.198), kind=kOutput, calls=%fused_computation.47 | convolution fusion | flops 884736 | bytes 147528 | tf_op jit(solution)/shard_map/ks,syi->kyi/dot_general | solution.py:85
  3.2 5.1 %collective-permute-start = (f32[3,32,128]{2,0,1:T(4,128)S(1)}, f32[3,32,128]{2,0,1:T(4,128)S(1)}, u32[]{:S(2)}, u32[]{:S(2)}) collective-permute-start(f32[3,32,128]{2,0,1:T(4,128)S(1)} %fusion.29), channel_id=1, source_target_pairs={{0,28},{4,0},{8,4},{12,8},{16,12},{20,16},{24,20},{28,24},{1,29},{... | collective-permute-start | bytes 147464 | tf_op jit(solution)/shard_map/ppermute | solution.py:13
  8.9 1.2 %fusion.27 = f32[3,32,128]{2,0,1:T(4,128)S(1)} fusion(f32[6,32,128]{2,1,0:T(8,128)} %bitcast.209, f32[3,6]{1,0:T(4,128)S(1)} %get-tuple-element.194), kind=kOutput, calls=%fused_computation.45 | convolution fusion | flops 884736 | bytes 147528 | tf_op jit(solution)/shard_map/ks,syi->kyi/dot_general | solution.py:85
  10.8 1.2 %fusion.25 = f32[3,32,128]{2,0,1:T(4,128)S(1)} fusion(f32[6,32,128]{2,1,0:T(8,128)} %bitcast.210, f32[3,6]{1,0:T(4,128)S(1)} %get-tuple-element.192), kind=kOutput, calls=%fused_computation.43 | convolution fusion | flops 884736 | bytes 147528 | tf_op jit(solution)/shard_map/ks,syi->kyi/dot_general | solution.py:85
  15.5 1.2 %fusion.10 = f32[1,31,31]{2,0,1:T(1,128)S(1)} fusion(f32[27,31,31]{2,1,0:T(8,128)S(1)} %copy-done, f32[1,27]{1,0:T(1,128)} %param.18), kind=kOutput, calls=%fused_computation.23 | convolution fusion | flops 311364 | bytes 107740 | tf_op jit(solution)/shard_map/k,kab->ab/dot_general | solution.py:133
  16.7 1.4 %fusion.3 = f32[31,128,128]{2,0,1:T(8,128)S(1)} fusion(pred[128,128,31]{1,0,2:T(32,128)(4,1)S(1)} %iota_compare_fusion, f32[1,31,31]{2,0,1:T(1,128)S(1)} %fusion.10), kind=kOutput, calls=%fused_computation.9 | convolution fusion | flops 188940288 | bytes 2543364 | tf_op jit(solution)/shard_map/jib,ab->aji/dot_general | solution.py:138
  18.1 1.1 %fusion.12 = f32[31,30,128]{2,0,1:T(8,128)} fusion(s32[30,128]{1,0:T(8,128)S(1)} %iota_subtract_fusion.1, f32[1,31,31]{2,0,1:T(1,128)S(1)} %fusion.10), kind=kOutput, calls=%fused_computation.26 | convolution fusion | flops 44401920 | bytes 495364 | tf_op jit(solution)/shard_map/jib,ab->aji/dot_general | solution.py:143
  21.3 4.2 %collective-permute-start.3 = (f32[19,768]{1,0:T(8,128)S(1)}, f32[19,768]{1,0:T(8,128)S(1)}, u32[]{:S(2)}, u32[]{:S(2)}) collective-permute-start(f32[19,768]{1,0:T(8,128)S(1)} %bitcast.225), channel_id=1, source_target_pairs={{0,1},{1,2},{2,3},{4,5},{5,6},{6,7},{8,9},{9,10},{10,11},{12,13},{... | collective-permute-start | bytes 175112 | tf_op jit(solution)/shard_map/ppermute | solution.py:21
  25.6 1.9 %collective-permute-start.4 = (f32[19,768]{1,0:T(8,128)S(1)}, f32[19,768]{1,0:T(8,128)S(1)}, u32[]{:S(2)}, u32[]{:S(2)}) collective-permute-start(f32[19,768]{1,0:T(8,128)S(1)} %bitcast.226), channel_id=1, source_target_pairs={{1,0},{2,1},{3,2},{5,4},{6,5},{7,6},{9,8},{10,9},{11,10},{13,12},{... | collective-permute-start | bytes 175112 | tf_op jit(solution)/shard_map/ppermute | solution.py:24
  27.6 3.7 %collective-permute-done.4 = f32[19,768]{1,0:T(8,128)S(1)} collective-permute-done((f32[19,768]{1,0:T(8,128)S(1)}, f32[19,768]{1,0:T(8,128)S(1)}, u32[]{:S(2)}, u32[]{:S(2)}) %collective-permute-start.4) | collective-permute-done | bytes 58400 | tf_op jit(solution)/shard_map/ppermute | solution.py:24
  33.4 50.5 %while.14 = (s32[]{:T(128)}, f32[32,6,128]{2,0,1:T(8,128)S(1)}, f32[62,896]{1,0:T(8,128)S(1)}, f32[31,128,128]{2,0,1:T(8,128)S(1)}, f32[31,30,128]{2,0,1:T(8,128)}, /*index=5*/s32[]{:T(128)}, s32[]{:T(128)}, s32[]{}) while((s32[]{:T(128)}, f32[32,6,128]{2,0,1:T(8,128)S(1)}, f32[62,896]{1,0:T(8,128)S(1)}, ...), condition=%wide.region_6.7_spmd.clone, body=%wide.region_5.6_spmd.clone.sunk | while | flops 46669828 | bytes 1347195 | solution.py:157
  33.9 0.9 constant_dynamic-slice_fusion.14
  35.5 0.9 constant_dynamic-slice_fusion.14
  43.6 0.9 constant_dynamic-slice_fusion.14
  48.5 0.9 constant_dynamic-slice_fusion.14
  53.4 0.9 constant_dynamic-slice_fusion.14
  58.3 0.9 constant_dynamic-slice_fusion.14
  63.2 0.9 constant_dynamic-slice_fusion.14
  74.6 0.9 constant_dynamic-slice_fusion.14
  79.5 0.9 constant_dynamic-slice_fusion.14
  84.4 1.5 %collective-permute-start.5 = (f32[3,32,128]{2,1,0:T(8,128)S(1)}, f32[3,32,128]{2,1,0:T(8,128)S(1)}, u32[]{:S(2)}, u32[]{:S(2)}) collective-permute-start(f32[3,32,128]{2,1,0:T(8,128)S(1)} %bitcast.229), channel_id=1, source_target_pairs={{0,4},{4,8},{8,12},{12,16},{16,20},{20,24},{24,28},{28,0},{1,5},{5... | collective-permute-start | bytes 147464 | tf_op jit(solution)/shard_map/ppermute | solution.py:13
  86.3 2.3 %collective-permute-start.7 = (f32[3,32,128]{2,1,0:T(8,128)S(1)}, f32[3,32,128]{2,1,0:T(8,128)S(1)}, u32[]{:S(2)}, u32[]{:S(2)}) collective-permute-start(f32[3,32,128]{2,1,0:T(8,128)S(1)} %bitcast.228), channel_id=1, source_target_pairs={{0,12},{4,16},{8,20},{12,24},{16,28},{20,0},{24,4},{28,8},{1,13},{... | collective-permute-start | bytes 147464 | tf_op jit(solution)/shard_map/ppermute | solution.py:13
  88.7 1.5 %collective-permute-done.5 = f32[3,32,128]{2,1,0:T(8,128)S(1)} collective-permute-done((f32[3,32,128]{2,1,0:T(8,128)S(1)}, f32[3,32,128]{2,1,0:T(8,128)S(1)}, u32[]{:S(2)}, u32[]{:S(2)}) %collective-permute-start.5) | collective-permute-done | bytes 49184 | tf_op jit(solution)/shard_map/ppermute | solution.py:13
  91.4 1.8 %collective-permute-done.6 = f32[3,32,128]{2,1,0:T(8,128)S(1)} collective-permute-done((f32[3,32,128]{2,1,0:T(8,128)S(1)}, f32[3,32,128]{2,1,0:T(8,128)S(1)}, u32[]{:S(2)}, u32[]{:S(2)}) %collective-permute-start.6) | collective-permute-done | bytes 49184 | tf_op jit(solution)/shard_map/ppermute | solution.py:13
  (269 shorter events, 53.6 us)
Async XLA Ops:
  0.0 15.5 %copy-start = (f32[27,31,31]{2,1,0:T(8,128)S(1)}, f32[27,31,31]{2,1,0:T(8,128)}, u32[]{:S(2)}) copy-start(f32[27,31,31]{2,1,0:T(8,128)} %param.17) | copy-start | bytes 311368
  3.2 17.7 %collective-permute-start = (f32[3,32,128]{2,0,1:T(4,128)S(1)}, f32[3,32,128]{2,0,1:T(4,128)S(1)}, u32[]{:S(2)}, u32[]{:S(2)}) collective-permute-start(f32[3,32,128]{2,0,1:T(4,128)S(1)} %fusion.29), channel_id=1, source_target_pairs={{0,28},{4,0},{8,4},{12,8},{16,12},{20,16},{24,20},{28,24},{1,29},{... | collective-permute-start | bytes 147464 | tf_op jit(solution)/shard_map/ppermute | solution.py:13
  10.1 10.9 %collective-permute-start.1 = (f32[3,32,128]{2,0,1:T(4,128)S(1)}, f32[3,32,128]{2,0,1:T(4,128)S(1)}, u32[]{:S(2)}, u32[]{:S(2)}) collective-permute-start(f32[3,32,128]{2,0,1:T(4,128)S(1)} %fusion.27), channel_id=1, source_target_pairs={{0,24},{4,28},{8,0},{12,4},{16,8},{20,12},{24,16},{28,20},{1,25},{... | collective-permute-start | bytes 147464 | tf_op jit(solution)/shard_map/ppermute | solution.py:13
  11.9 9.0 %collective-permute-start.2 = (f32[3,32,128]{2,0,1:T(4,128)S(1)}, f32[3,32,128]{2,0,1:T(4,128)S(1)}, u32[]{:S(2)}, u32[]{:S(2)}) collective-permute-start(f32[3,32,128]{2,0,1:T(4,128)S(1)} %fusion.25), channel_id=1, source_target_pairs={{0,20},{4,24},{8,28},{12,0},{16,4},{20,8},{24,12},{28,16},{1,21},{... | collective-permute-start | bytes 147464 | tf_op jit(solution)/shard_map/ppermute | solution.py:13
  15.1 4.5 %copy-start.3 = (s32[1,6]{1,0:T(1,128)S(1)}, s32[1,6]{1,0:T(1,128)}, u32[]{:S(2)}) copy-start(s32[1,6]{1,0:T(1,128)} %param.16) | copy-start | bytes 76
  15.4 4.5 %copy-start.1 = (f32[1,6,32,128]{3,2,1,0:T(8,128)S(1)}, f32[1,6,32,128]{3,2,1,0:T(8,128)}, u32[]{:S(2)}) copy-start(f32[1,6,32,128]{3,2,1,0:T(8,128)} %param.12) | copy-start | bytes 294916
  15.4 4.8 %copy-start.2 = (f32[1,32,768]{2,1,0:T(8,128)S(1)}, f32[1,32,768]{2,1,0:T(8,128)}, u32[]{:S(2)}) copy-start(f32[1,32,768]{2,1,0:T(8,128)} %param.11) | copy-start | bytes 294916
  21.3 6.2 %collective-permute-start.3 = (f32[19,768]{1,0:T(8,128)S(1)}, f32[19,768]{1,0:T(8,128)S(1)}, u32[]{:S(2)}, u32[]{:S(2)}) collective-permute-start(f32[19,768]{1,0:T(8,128)S(1)} %bitcast.225), channel_id=1, source_target_pairs={{0,1},{1,2},{2,3},{4,5},{5,6},{6,7},{8,9},{9,10},{10,11},{12,13},{... | collective-permute-start | bytes 175112 | tf_op jit(solution)/shard_map/ppermute | solution.py:21
  25.6 5.7 %collective-permute-start.4 = (f32[19,768]{1,0:T(8,128)S(1)}, f32[19,768]{1,0:T(8,128)S(1)}, u32[]{:S(2)}, u32[]{:S(2)}) collective-permute-start(f32[19,768]{1,0:T(8,128)S(1)} %bitcast.226), channel_id=1, source_target_pairs={{1,0},{2,1},{3,2},{5,4},{6,5},{7,6},{9,8},{10,9},{11,10},{13,12},{... | collective-permute-start | bytes 175112 | tf_op jit(solution)/shard_map/ppermute | solution.py:24
  84.4 5.9 %collective-permute-start.5 = (f32[3,32,128]{2,1,0:T(8,128)S(1)}, f32[3,32,128]{2,1,0:T(8,128)S(1)}, u32[]{:S(2)}, u32[]{:S(2)}) collective-permute-start(f32[3,32,128]{2,1,0:T(8,128)S(1)} %bitcast.229), channel_id=1, source_target_pairs={{0,4},{4,8},{8,12},{12,16},{16,20},{20,24},{24,28},{28,0},{1,5},{5... | collective-permute-start | bytes 147464 | tf_op jit(solution)/shard_map/ppermute | solution.py:13
  86.3 4.9 %collective-permute-start.7 = (f32[3,32,128]{2,1,0:T(8,128)S(1)}, f32[3,32,128]{2,1,0:T(8,128)S(1)}, u32[]{:S(2)}, u32[]{:S(2)}) collective-permute-start(f32[3,32,128]{2,1,0:T(8,128)S(1)} %bitcast.228), channel_id=1, source_target_pairs={{0,12},{4,16},{8,20},{12,24},{16,28},{20,0},{24,4},{28,8},{1,13},{... | collective-permute-start | bytes 147464 | tf_op jit(solution)/shard_map/ppermute | solution.py:13
  88.5 4.7 %collective-permute-start.6 = (f32[3,32,128]{2,1,0:T(8,128)S(1)}, f32[3,32,128]{2,1,0:T(8,128)S(1)}, u32[]{:S(2)}, u32[]{:S(2)}) collective-permute-start(f32[3,32,128]{2,1,0:T(8,128)S(1)} %bitcast.227), channel_id=1, source_target_pairs={{0,8},{4,12},{8,16},{12,20},{16,24},{20,28},{24,0},{28,4},{1,9},{5... | collective-permute-start | bytes 147464 | tf_op jit(solution)/shard_map/ppermute | solution.py:13
where the time goes:
time: 95.3 us; the launch traced here: 94.3 us
  local copies, waits for them, and re-layouts  38.3 us (40%)
  matrix products  25.2 us (26%)
  starting transfers between devices  15.6 us (16%)
  waiting for transfers between devices  7.61 us (8%)
  other arithmetic  4.58 us (5%)
  loops' own time  1.73 us (2%)
  between operations  1.14 us (1%)
    dynamic_slice x31, local copies, waits for them, and re-layouts, kernel_row(): lax.dynamic_index_in_dim(trail_bands, tap_row, 0, keepdims=False)  28.6 us
    ppermute x6, starting transfers between devices, shifted(): return lax.ppermute(value, axis, pairs)  9.47 us
    dot_general x31, matrix products, kernel_row(): jnp.einsum('ycj,ji->yci', main_part, lead_now, precision=highest)  7.33 us
    dot_general x31, matrix products, kernel_row(): jnp.einsum('ycj,ji->yci', next_part, trail_now, precision=highest)  6.7 us
    ppermute x1, starting transfers between devices, with_halo(): lax.ppermute(lax.slice_in_dim(block, block.shape[dim] - width, None, axis...  4.24 us
    ppermute x6, waiting for transfers between devices, shifted(): return lax.ppermute(value, axis, pairs)  3.91 us
    dot_general x4, matrix products, body(): jnp.einsum('ks,syi->kyi', routings[reach], stored, precision=highest)  3.83 us
    ppermute x1, waiting for transfers between devices, with_halo(): lax.ppermute(lax.slice_in_dim(block, 0, width, axis=dim), axis, backward)  3.7 us
  transfers between devices with their start and end apart: 8, of which 4 were waited for; matrix products, arithmetic and copies ran while one was open for 13% of the time, Pallas kernels for 0%

commit v1 on v0

v1 whole, which is shorter than its diff:
```python
import jax
import jax.numpy as jnp
from jax import lax
from jax.experimental import pallas as pl
from jax.experimental.pallas import tpu as pltpu
from jax.sharding import PartitionSpec as P

SPAN = 4
LONG = 3
LANES = 128
ABOVE = 16
BELOW = 24
EDGE = 32
SPLIT = 8


def fdiv(value, divisor, bound):
    factor = 65536 // divisor + 1
    assert bound * (factor * divisor - 65536) < 65536
    return (value * factor) >> 16


def run_info(sources, row, slots, dets):
    columns = sources.shape[1]
    reach = []
    for c in range(columns):
        owner = fdiv(sources[row, c], slots, dets * slots)
        step = owner - row
        reach.append(jnp.where(step < 0, step + dets, step))
    starts, lengths = [], []
    for j in range(SPAN):
        starts.append(sum((x < j).astype(jnp.int32) for x in reach))
        lengths.append(sum((x == j).astype(jnp.int32) for x in reach))
    return starts, lengths


def wrap(value, count):
    return jnp.where(value < 0, value + count, value)


def lane_ids(rows):
    return lax.broadcasted_iota(jnp.int32, (rows, LANES), 1)


def row_ids(rows):
    return lax.broadcasted_iota(jnp.int32, (rows, LANES), 0)


def prep_body(dets, where, src, off, sw, valid, coef, back, sci, tmpl, basis,
              out_a, out_b, out_3, out_2, out_0, halo_a, halo_b, kern):
    d = where[0]
    r = where[1]
    slots, band = tmpl.shape[0], tmpl.shape[1]
    columns = src.shape[1]
    even_d = lax.rem(d, 2) == 0
    even_r = lax.rem(r, 2) == 0
    starts, lengths = run_info(src, d, slots, dets)
    grow = row_ids(band) + r * band

    tiles = []
    for j in range(SPAN):
        mine = []
        for k in range(LONG):
            c = jnp.minimum(starts[j] + k, columns - 1)
            limit = jnp.where(k < lengths[j], valid[0, c], 0)
            block = sci[:, pl.ds(pl.multiple_of(c * LANES, LANES), LANES)]
            mine.append(jnp.where(grow < limit, block - back[0], 0.0))
        tiles.append(mine)

    width = basis.shape[1]
    total = coef[0, 0] * basis[0]
    for k in range(1, basis.shape[0]):
        total = total + coef[0, k] * basis[k]
    kern[...] = jnp.zeros_like(kern)
    kern[0:width, 0:width] = total
    flip = jnp.transpose(kern[...])
    packed = flip[0:8]
    for g in range(1, 4):
        packed = packed + pltpu.roll(flip[8 * g:8 * g + 8], EDGE * g, 1)

    lane8 = lane_ids(8)
    row8 = row_ids(8)
    params = jnp.zeros((8, LANES), jnp.float32)
    for c in range(columns):
        line = jnp.where(lane8 == 0, off[0, 0, c].astype(jnp.float32), 0.0)
        line = jnp.where(lane8 == 1, off[1, 0, c].astype(jnp.float32), line)
        line = jnp.where(lane8 == 2, sw[0, 0, c], line)
        line = jnp.where(lane8 == 3, sw[1, 0, c], line)
        line = jnp.where(lane8 == 4, valid[0, c].astype(jnp.float32), line)
        params = jnp.where(row8 == c, line, params)

    lane = lane_ids(band)
    left = jnp.zeros((band, LANES), jnp.float32)
    right = jnp.zeros((band, LANES), jnp.float32)
    for q in range(SPAN - 1):
        other = wrap(d - q, dets)
        st, ln = run_info(src, other, slots, dets)
        s = src[other, st[q] + ln[q] - 1] - d * slots
        piece = pltpu.roll(tmpl[s], (EDGE * q + EDGE) % LANES, 1)
        left = jnp.where((lane >= EDGE * q) & (lane < EDGE * q + EDGE), piece, left)
        other = wrap(d - q - 1, dets)
        st, ln = run_info(src, other, slots, dets)
        s = src[other, st[q + 1]] - d * slots
        piece = tmpl[s]
        if q:
            piece = pltpu.roll(piece, EDGE * q, 1)
        right = jnp.where((lane >= EDGE * q) & (lane < EDGE * q + EDGE), piece, right)

    def fill(ref, j):
        for k in range(LONG):
            ref[band * k:band * k + band] = tiles[j][k]
        ref[band * LONG:band * LONG + 8] = packed
        ref[band * LONG + 8:band * LONG + 16] = params

    fill(out_0, 0)
    fill(out_2, 2)
    fill(out_3, 3)

    def pair(plus, minus):
        fill(plus, 1)
        plus[band * LONG + 16:band * LONG + 16 + band] = left
        minus[0:band * LONG + 16] = jnp.zeros((band * LONG + 16, LANES), jnp.float32)
        minus[band * LONG + 16:band * LONG + 16 + band] = right

    @pl.when(even_d)
    def _():
        pair(out_a, out_b)

    @pl.when(jnp.logical_not(even_d))
    def _():
        pair(out_b, out_a)

    for s in range(slots):
        top = tmpl[s, 0:BELOW]
        bottom = tmpl[s, band - BELOW:band]
        halo_a[:, LANES * s:LANES * s + LANES] = jnp.where(even_r, bottom, top)
        halo_b[:, LANES * s:LANES * s + LANES] = jnp.where(even_r, top, bottom)


def pack_body(band, slots, where, got_a, got_b, in_a, in_b, halo_a, halo_b):
    halo_a[:, 0:LANES * slots] = in_a[...]
    halo_b[:, 0:LANES * slots] = in_b[...]
    d = where[0]
    r = where[1]
    even_d = lax.rem(d, 2) == 0
    even_r = lax.rem(r, 2) == 0
    base = got_a.shape[0] - band
    from_a = got_a[base:base + band]
    from_b = got_b[base:base + band]
    left = jnp.where(even_d, from_b, from_a)
    right = jnp.where(even_d, from_a, from_b)
    for i, strip in enumerate((left, right)):
        at = LANES * (slots + i)
        top = strip[0:BELOW]
        bottom = strip[band - BELOW:band]
        halo_a[:, at:at + LANES] = jnp.where(even_r, bottom, top)
        halo_b[:, at:at + LANES] = jnp.where(even_r, top, bottom)


def main_body(dets, where, src, tmpl, own, got_a, got_b, got_2, got_3, halo_a, halo_b, out,
              plus, minus, scal, sem, tiles, lefts, rights, kpad, rho, vmat, ws, wt, acc, sacc, tr):
    d = where[0]
    r = where[1]
    slots, band = tmpl.shape[0], tmpl.shape[1]
    columns = src.shape[1]
    even_d = lax.rem(d, 2) == 0
    even_r = lax.rem(r, 2) == 0
    base = got_a.shape[0] - band
    tpad = LANES + 8
    spad = EDGE + 8

    @pl.when(even_d)
    def _():
        plus[...] = got_b[...]
        minus[...] = got_a[base:base + band]

    @pl.when(jnp.logical_not(even_d))
    def _():
        plus[...] = got_a[...]
        minus[...] = got_b[base:base + band]

    packets = [own, plus, got_2, got_3]
    copies = []
    for j in range(SPAN):
        copies.append(pltpu.make_async_copy(
            packets[j].at[pl.ds(band * LONG + 8, 8), :], scal.at[j], sem.at[j]))
        copies[-1].start()

    def stacked(middle, at):
        up_a = halo_a[BELOW - ABOVE:BELOW, at:at + LANES]
        up_b = halo_b[BELOW - ABOVE:BELOW, at:at + LANES]
        dn_a = halo_a[:, at:at + LANES]
        dn_b = halo_b[:, at:at + LANES]
        up = jnp.where(even_r, up_b, up_a)
        down = jnp.where(even_r, dn_a, dn_b)
        return jnp.transpose(jnp.concatenate([up, middle, down], axis=0))

    tall = ABOVE + band + BELOW
    for s in range(slots):
        t = stacked(tmpl[s], LANES * s)
        tiles[tpad * s:tpad * s + LANES, 0:tall] = t
        tiles[tpad * s + LANES:tpad * s + tpad, 0:tall] = jnp.broadcast_to(t[LANES - 1:LANES], (8, tall))
    t = stacked(plus[base:base + band], LANES * slots)
    for q in range(SPAN - 1):
        lefts[spad * q:spad * q + EDGE, 0:tall] = t[EDGE * q:EDGE * q + EDGE]
        lefts[spad * q + EDGE:spad * q + spad, 0:tall] = jnp.broadcast_to(
            t[EDGE * q + EDGE - 1:EDGE * q + EDGE], (8, tall))
    rights[:, 0:tall] = stacked(minus[...], LANES * (slots + 1))

    lane = lane_ids(8)
    kpad[...] = jnp.zeros_like(kpad)
    for j in range(SPAN):
        pk = packets[j][band * LONG:band * LONG + 8]
        back = (EDGE - lane // 4) % EDGE
        for g in range(4):
            kpad[8 + 8 * g:16 + 8 * g] = jnp.take_along_axis(pk, back + EDGE * g, axis=1)
        line = jnp.zeros((40, LANES), jnp.float32)
        dx = lane_ids(40) % 4
        for k in range(4):
            line = jnp.where(dx == k, kpad[8 - k:48 - k], line)
        rho[...] = line
        keep = (lane_ids(EDGE) // 4) <= row_ids(EDGE)
        for u in range(36):
            one = jnp.broadcast_to(rho[u:u + 1], (EDGE, LANES))
            one = pltpu.roll(one, 0, 1, stride=4, stride_axis=0)
            high = one.astype(jnp.bfloat16).astype(jnp.float32)
            low = one - high
            at = 64 * u
            vmat[j, at:at + EDGE, 0:LANES] = jnp.where(keep, high, 0.0).astype(jnp.bfloat16)
            vmat[j, at + EDGE:at + 64, 0:LANES] = jnp.where(keep, 0.0, high).astype(jnp.bfloat16)
            vmat[j, at:at + EDGE, LANES:2 * LANES] = jnp.where(keep, low, 0.0).astype(jnp.bfloat16)
            vmat[j, at + EDGE:at + 64, LANES:2 * LANES] = jnp.where(keep, 0.0, low).astype(jnp.bfloat16)

    acc[...] = jnp.zeros_like(acc)
    sacc[...] = jnp.zeros_like(sacc)
    ws[...] = jnp.zeros_like(ws)
    for c in copies:
        c.wait()

    def warp(j, c, ref, at, count, dst):
        ro = scal[j, c, 0].astype(jnp.int32)
        co = scal[j, c, 1].astype(jnp.int32)
        rw = scal[j, c, 2]
        cw = scal[j, c, 3]
        one = ref[pl.ds(at + co, count), :]
        two = ref[pl.ds(at + co + 1, count), :]
        mix = (1.0 - cw) * one + cw * two
        upper = pltpu.roll(mix, LANES - 1 - ro, 1)
        lower = pltpu.roll(mix, LANES - 2 - ro, 1)
        both = (1.0 - rw) * upper + rw * lower
        ids = lane_ids(count)
        grow = ids + (r * band - (ABOVE - 1))
        ok = (ids < 64) & (grow >= 0) & (grow < LANES)
        ws[pl.ds(dst, count), :] = jnp.where(ok, both, 0.0)

    def conv(j, rows):
        total = jnp.zeros((2 * rows, 2 * LANES), jnp.float32)
        for t in range(9):
            one = wt[pl.ds(9 + 4 * t, rows, stride=4), :]
            two = wt[pl.ds(11 + 4 * t, rows, stride=4), :]
            lhs = jnp.concatenate([one, two], axis=1)
            high = lhs.astype(jnp.bfloat16)
            low = (lhs - high.astype(jnp.float32)).astype(jnp.bfloat16)
            total = total + jnp.dot(
                jnp.concatenate([high, low], axis=0), vmat[j, 256 * t:256 * t + 256],
                preferred_element_type=jnp.float32)
        res = total[0:rows] + total[rows:2 * rows]
        return res[:, 0:LANES] + res[:, LANES:2 * LANES]

    tally = [jnp.int32(0) for _ in range(slots)]
    for j in range(SPAN):
        det = wrap(d - j, dets)
        st, ln = run_info(src, det, slots, dets)
        st, ln = st[j], ln[j]
        s0 = src[det, st] - d * slots
        for s in range(slots):
            tally[s] = tally[s] + ((s0 <= s) & (s < s0 + ln)).astype(jnp.int32)
        if j > 0:
            warp(j, st - 1, lefts, spad * (j - 1) + EDGE - 16, 16, 8)
        else:
            ws[8:24] = jnp.zeros((16, LANES), jnp.float32)
        end = pl.multiple_of(24 + LANES * ln, 8)
        if j < SPAN - 1:
            warp(j, jnp.minimum(st + ln, columns - 1), rights, EDGE * j, 16, end)
        else:
            ws[pl.ds(end, 16), :] = jnp.zeros((16, LANES), jnp.float32)

        def finish(count, j=j, st=st, s0=s0):
            for k in range(count):
                warp(j, st + k, tiles, (s0 + k) * tpad, LANES, 24 + LANES * k)
            n = LANES * count + 40
            wt[pl.ds(8, n), :] = ws[pl.ds(8, n), :] + pltpu.roll(ws[pl.ds(9, n), :], 64, 1)
            res = conv(j, EDGE * count)
            ids = lane_ids(EDGE) // 4 + r * band
            for k in range(count):
                limit = scal[j, st + k, 4].astype(jnp.int32)
                piece = jnp.where(ids < limit, res[EDGE * k:EDGE * k + EDGE], 0.0)
                at = pl.multiple_of((s0 + k) * EDGE, EDGE)
                acc[pl.ds(at, EDGE), :] += piece
                sacc[pl.ds(at, EDGE), :] += packets[j][band * k:band * k + band]

        @pl.when(ln == 1)
        def _():
            finish(1)

        @pl.when(ln != 1)
        def _():
            finish(LONG)

    for g in range(0, slots, 4):
        tr[...] = jnp.transpose(acc[EDGE * g:EDGE * g + LANES])
        planes = [tr[pl.ds(k, EDGE, stride=4), :] for k in range(4)]
        ids = lane_ids(EDGE)
        for s in range(g, min(g + 4, slots)):
            pick = ids // 4 + EDGE * (s - g)
            image = jnp.zeros((EDGE, LANES), jnp.float32)
            for k in range(4):
                image = jnp.where(ids % 4 == k, jnp.take_along_axis(planes[k], pick, axis=1), image)
            scale = jnp.float32(1.0)
            for n in range(2, SPAN + 1):
                scale = jnp.where(tally[s] == n, jnp.float32(1.0 / n), scale)
            out[s] = (sacc[EDGE * s:EDGE * s + EDGE] - image) * scale


def shifted(value, axis, steps):
    count = lax.axis_size(axis)
    return lax.ppermute(value, axis, [(i, (i + steps) % count) for i in range(count)])


def paired(value, axis, first, ring):
    count = lax.axis_size(axis)
    pairs = []
    for i in range(first, count if ring else count - 1, 2):
        k = (i + 1) % count
        pairs += [(i, k), (k, i)]
    return lax.ppermute(value, axis, pairs)


def body(science, template, tile_source, offsets, shift_weights, valid_rows, basis_kernels,
         coefficients, background):
    f32 = jnp.float32
    dets = lax.axis_size("det")
    assert dets % 2 == 0 and dets >= SPAN
    slots, band, tile = template.shape[1:]
    assert tile == LANES and band == EDGE
    where = jnp.stack([lax.axis_index("det"), lax.axis_index("row")]).astype(jnp.int32)
    vm = pl.BlockSpec(memory_space=pltpu.VMEM)
    sm = pl.BlockSpec(memory_space=pltpu.SMEM)
    rows = band * LONG + 16
    shapes = [(rows + band, LANES)] * 2 + [(rows, LANES)] * 3 + [(BELOW, LANES * slots)] * 2
    out_a, out_b, out_3, out_2, own, halo_a, halo_b = pl.pallas_call(
        lambda *refs: prep_body(dets, *refs),
        out_shape=[jax.ShapeDtypeStruct(s, f32) for s in shapes],
        in_specs=[sm] * 7 + [vm] * 3,
        out_specs=[vm] * len(shapes),
        scratch_shapes=[pltpu.VMEM((LANES, LANES), f32)],
        name="prep",
    )(where, tile_source, offsets, shift_weights, valid_rows, coefficients, background,
      science[0], template[0], basis_kernels)
    got_b = paired(out_b, "det", 1, True)
    got_a = paired(out_a, "det", 0, False)
    got_3 = shifted(out_3, "det", 3)
    got_2 = shifted(out_2, "det", 2)
    halo_a, halo_b = pl.pallas_call(
        lambda *refs: pack_body(band, slots, *refs),
        out_shape=[jax.ShapeDtypeStruct((BELOW, LANES * (slots + 2)), f32)] * 2,
        in_specs=[sm] + [vm] * 4,
        out_specs=[vm] * 2,
        name="pack",
    )(where, got_a, got_b, halo_a, halo_b)
    halo_a = paired(halo_a, "row", 0, False)
    halo_b = paired(halo_b, "row", 1, False)
    groups = -(-slots // 4) * 4
    out = pl.pallas_call(
        lambda *refs: main_body(dets, *refs),
        out_shape=jax.ShapeDtypeStruct((slots, band, LANES), f32),
        in_specs=[sm] * 2 + [vm] * 8,
        out_specs=vm,
        scratch_shapes=[
            pltpu.VMEM((rows + band, LANES), f32),
            pltpu.VMEM((band, LANES), f32),
            pltpu.SMEM((SPAN, 8, LANES), f32),
            pltpu.SemaphoreType.DMA((SPAN,)),
            pltpu.VMEM(((LANES + 8) * slots + 8, LANES), f32),
            pltpu.VMEM(((EDGE + 8) * (SPAN - 1) + 8, LANES), f32),
            pltpu.VMEM((LANES, LANES), f32),
            pltpu.VMEM((48, LANES), f32),
            pltpu.VMEM((40, LANES), f32),
            pltpu.VMEM((SPAN, 36 * 64, 2 * LANES), jnp.bfloat16),
            pltpu.VMEM((LANES * LONG + 72, LANES), f32),
            pltpu.VMEM((LANES * LONG + 72, LANES), f32),
            pltpu.VMEM((EDGE * groups, LANES), f32),
            pltpu.VMEM((EDGE * groups, LANES), f32),
            pltpu.VMEM((LANES, LANES), f32),
        ],
        name="subtract",
    )(where, tile_source, template[0], own, got_a, got_b, got_2, got_3, halo_a, halo_b)
    return out[None]


def solution(mesh):
    in_specs = (
        P("det", "row", None),
        P("det", None, "row", None),
        P(),
        P(None, "det", None),
        P(None, "det", None),
        P("det", None),
        P(),
        P("det", None),
        P("det"),
    )
    out_specs = P("det", None, "row", None)
    return jax.shard_map(body, mesh=mesh, in_specs=in_specs, out_specs=out_specs, check_vma=False)
```

time: 95.3 us -> 32.7 us (0.34)
  local copies, waits for them, and re-layouts: 38.3 us -> 1.31 us
  matrix products: 25.2 us -> 0 us
  Pallas kernels: 0 us -> 10.3 us
  starting transfers between devices: 15.6 us -> 11.4 us
  other arithmetic: 4.58 us -> 0.65 us
  loops' own time: 1.73 us -> 0 us
    dynamic_slice x62 -> x0, local copies, waits for them, and re-layouts: 31 us -> none  [the longest x31 28.6 us: kernel_row(): lax.dynamic_index_in_dim(trail_bands, tap_row, 0, keepdims=False)]
    dot_general x81 -> x0, matrix products: 25.2 us -> none  [the longest x31 7.33 us: kernel_row(): jnp.einsum('ycj,ji->yci', main_part, lead_now, precision=highest)]
    pallas_call x0 -> x3, Pallas kernels: none -> 10.3 us  [the longest x1 6.5 us: body(): pl.pallas_call(lambda *refs: main_body(dets, *refs), out_shape=jax.ShapeD...]
    ppermute x8 -> x6, starting transfers between devices: 15.6 us -> 11.4 us  [the longest x4 10.4 us: paired(): return lax.ppermute(value, axis, pairs)]
    slice x40 -> x0, local copies, waits for them, and re-layouts: 4.05 us -> none  [the longest x31 3.2 us: kernel_row(): rows_here[:, tile_size:].reshape(band_rows, tile_count, tile_size)]
    another operation x1 -> x0, loops' own time: 1.73 us -> none  [body(): lax.fori_loop(0, kernel_width, kernel_row, jnp.zeros((band_rows, tile_cou...]
    eq x7 -> x0, other arithmetic: 1.2 us -> none  [the longest x1 0.85 us: send_routing(): owners == det_index]
    ppermute x8 -> x6, waiting for transfers between devices: 7.61 us -> 7.96 us  [the longest x2 5.11 us: shifted(): lax.ppermute(value, axis, [(i, (i + steps) % count) for i in range(count)])]
  transfers between devices with their start and end apart: 8 -> 6, of which waited for: 4 -> 3; matrix products, arithmetic and copies ran while one was open for 13% -> 0% of each run, Pallas kernels for 0% -> 0%
where the time goes in v1:
time: 32.7 us; the launch traced here: 32.4 us
  starting transfers between devices  11.4 us (35%)
  Pallas kernels  10.3 us (31%)
  waiting for transfers between devices  7.96 us (24%)
  local copies, waits for them, and re-layouts  1.31 us (4%)
  between operations  0.72 us (2%)
  other arithmetic  0.65 us (2%)
    ppermute x4, starting transfers between devices, paired(): return lax.ppermute(value, axis, pairs)  10.4 us
    pallas_call x1, Pallas kernels, body(): pl.pallas_call(lambda *refs: main_body(dets, *refs), out_shape=jax.ShapeD...  6.5 us
    ppermute x2, waiting for transfers between devices, shifted(): lax.ppermute(value, axis, [(i, (i + steps) % count) for i in range(count)])  5.11 us
    ppermute x4, waiting for transfers between devices, paired(): return lax.ppermute(value, axis, pairs)  2.85 us
    pallas_call x1, Pallas kernels, body(): pl.pallas_call(lambda *refs: prep_body(dets, *refs), out_shape=[jax.Shape...  2.14 us
    pallas_call x1, Pallas kernels, body(): pl.pallas_call(lambda *refs: pack_body(band, slots, *refs), out_shape=[ja...  1.7 us
    unnamed x16, local copies, waits for them, and re-layouts  1.31 us
    ppermute x2, starting transfers between devices, shifted(): lax.ppermute(value, axis, [(i, (i + steps) % count) for i in range(count)])  0.98 us
  transfers between devices with their start and end apart: 6, of which 3 were waited for; matrix products, arithmetic and copies ran while one was open for 0% of the time, Pallas kernels for 0%

profile of v1, /device:TPU:1, one launch (start us, length us, event | category | flops | bytes accessed | tf_op | source)
XLA Modules:
  0.0 32.4 jit_solution(11712836988663403567)
XLA Ops:
  0.7 0.6 %pad_add_fusion.refs_0_ = s32[2]{0:T(128)} fusion(s32[1]{0:T(128)} %bitcast.1, s32[1]{0:T(128)} %bitcast), kind=kLoop, calls=%fused_computation | loop fusion | flops 2 | bytes 16 | tf_op jit(solution)/shard_map/stack | solution.py:346
  1.3 2.1 %prep.1 = (f32[144,128]{1,0:T(8,128)}, f32[144,128]{1,0:T(8,128)}, f32[112,128]{1,0:T(8,128)}, f32[112,128]{1,0:T(8,128)}, f32[112,128]{1,0:T(8,128)}, /*index=5*/f32[24,768]{1,0:T(8,128)}, f32[24,768]{1,0:T(8,128)}) custom-call(s32[2]{0:T(128)} %pad_add_fusion.refs_0_, s32[8,6]{1,0:T(8,128)} %refs_1_.3, s32[2,1,6]{2,1,0:T(1,128)} %refs_2_.1, ...), custom_call_target="tpu_custom_call" | custom-call | tf_op jit(solution)/shard_map/prep/pallas_call | solution.py:351
  3.4 2.1 %collective-permute-start = (f32[144,128]{1,0:T(8,128)}, f32[144,128]{1,0:T(8,128)S(1)}, u32[]{:S(2)}, u32[]{:S(2)}) collective-permute-start(f32[144,128]{1,0:T(8,128)} %get-tuple-element.15), channel_id=1, source_target_pairs={{0,4},{4,0},{8,12},{12,8},{16,20},{20,16},{24,28},{28,24},{1,5},{5... | collective-permute-start | bytes 221192 | tf_op jit(solution)/shard_map/ppermute | solution.py:336
  5.5 3.3 %collective-permute-start.1 = (f32[144,128]{1,0:T(8,128)}, f32[144,128]{1,0:T(8,128)S(1)}, u32[]{:S(2)}, u32[]{:S(2)}) collective-permute-start(f32[144,128]{1,0:T(8,128)} %get-tuple-element.16), channel_id=1, source_target_pairs={{4,8},{8,4},{12,16},{16,12},{20,24},{24,20},{28,0},{0,28},{5,9},{9... | collective-permute-start | bytes 221192 | tf_op jit(solution)/shard_map/ppermute | solution.py:336
  8.8 0.0 collective-permute-done.refs_1_.refs_4_
  8.8 2.8 %collective-permute-done.1.refs_2_.refs_5_ = f32[144,128]{1,0:T(8,128)S(1)} collective-permute-done((f32[144,128]{1,0:T(8,128)}, f32[144,128]{1,0:T(8,128)S(1)}, u32[]{:S(2)}, u32[]{:S(2)}) %collective-permute-start.1) | collective-permute-done | bytes 73760 | tf_op jit(solution)/shard_map/ppermute | solution.py:336
  11.6 0.0 copy-done
  11.6 0.6 %copy-done.1 = f32[144,128]{1,0:T(8,128)} copy-done((f32[144,128]{1,0:T(8,128)}, f32[144,128]{1,0:T(8,128)S(1)}, u32[]{:S(2)}) %copy-start.1) | copy-done | bytes 73752
  12.2 1.7 %pack.1 = (f32[24,1024]{1,0:T(8,128)}, f32[24,1024]{1,0:T(8,128)}) custom-call(s32[2]{0:T(128)} %pad_add_fusion.refs_0_, f32[144,128]{1,0:T(8,128)} %copy-done, f32[144,128]{1,0:T(8,128)} %copy-done.1, f32[24,768]{1,0:T(8,128)} %get-tuple-element.19.refs_3_, f32[24,768]{1,0:T(8,128)} %get-tuple-element.20.refs_4_), custom_call_target="tpu_custom_call" | custom-call | tf_op jit(solution)/shard_map/pack/pallas_call | solution.py:364
  13.9 2.1 %collective-permute-start.4 = (f32[24,1024]{1,0:T(8,128)}, f32[24,1024]{1,0:T(8,128)S(1)}, u32[]{:S(2)}, u32[]{:S(2)}) collective-permute-start(f32[24,1024]{1,0:T(8,128)} %get-tuple-element.21), channel_id=1, source_target_pairs={{0,1},{1,0},{2,3},{3,2},{4,5},{5,4},{6,7},{7,6},{8,9},{9,8},{10,11... | collective-permute-start | bytes 294920 | tf_op jit(solution)/shard_map/ppermute | solution.py:336
  16.0 3.0 %collective-permute-start.5 = (f32[24,1024]{1,0:T(8,128)}, f32[24,1024]{1,0:T(8,128)S(1)}, u32[]{:S(2)}, u32[]{:S(2)}) collective-permute-start(f32[24,1024]{1,0:T(8,128)} %get-tuple-element.22), channel_id=1, source_target_pairs={{1,2},{2,1},{5,6},{6,5},{9,10},{10,9},{13,14},{14,13},{17,18},{18,... | collective-permute-start | bytes 294920 | tf_op jit(solution)/shard_map/ppermute | solution.py:336
  19.0 0.0 copy-done.7
  19.1 0.1 collective-permute-start.2
  19.1 0.0 copy-done.6
  19.1 0.9 %collective-permute-start.3 = (f32[112,128]{1,0:T(8,128)S(1)}, f32[112,128]{1,0:T(8,128)S(1)}, u32[]{:S(2)}, u32[]{:S(2)}) collective-permute-start(f32[112,128]{1,0:T(8,128)S(1)} %copy-done.6), channel_id=1, source_target_pairs={{0,12},{4,16},{8,20},{12,24},{16,28},{20,0},{24,4},{28,8},{1,13},{... | collective-permute-start | bytes 172040 | tf_op jit(solution)/shard_map/ppermute | solution.py:327
  20.1 3.9 %collective-permute-done.2.refs_6_ = f32[112,128]{1,0:T(8,128)S(1)} collective-permute-done((f32[112,128]{1,0:T(8,128)S(1)}, f32[112,128]{1,0:T(8,128)S(1)}, u32[]{:S(2)}, u32[]{:S(2)}) %collective-permute-start.2) | collective-permute-done | bytes 57376 | tf_op jit(solution)/shard_map/ppermute | solution.py:327
  23.9 1.2 %collective-permute-done.3.refs_7_ = f32[112,128]{1,0:T(8,128)S(1)} collective-permute-done((f32[112,128]{1,0:T(8,128)S(1)}, f32[112,128]{1,0:T(8,128)S(1)}, u32[]{:S(2)}, u32[]{:S(2)}) %collective-permute-start.3) | collective-permute-done | bytes 57376 | tf_op jit(solution)/shard_map/ppermute | solution.py:327
  25.2 0.0 collective-permute-done.4.refs_8_
  25.2 0.0 collective-permute-done.5.refs_9_
  25.2 0.0 copy-start.3
  25.2 0.6 %copy-done.5 = f32[112,128]{1,0:T(8,128)} copy-done((f32[112,128]{1,0:T(8,128)}, f32[112,128]{1,0:T(8,128)S(1)}, u32[]{:S(2)}) %copy-start.5) | copy-done | bytes 57368
  25.8 0.1 copy-done.2
  25.8 0.0 copy-done.3
  25.9 6.5 %subtract.1 = f32[6,32,128]{2,1,0:T(8,128)} custom-call(s32[2]{0:T(128)} %pad_add_fusion.refs_0_, s32[8,6]{1,0:T(8,128)} %refs_1_.3, f32[6,32,128]{2,1,0:T(8,128)} %bitcast.6, f32[112,128]{1,0:T(8,128)} %get-tuple-element.14.refs_3_, f32[144,128]{1,0:T(8,128)} %copy-done, f32[144,128]{1,0:T(8,128)} %copy-done.1, f32[112,128]{1,0:T(8,128)} %copy-done.4, ...), custom_call_target="tpu_custom_call" | custom-call | tf_op jit(solution)/shard_map/subtract/pallas_call | solution.py:374
  (8 shorter events, 0.0 us)
Async XLA Ops:
  3.4 5.3 %collective-permute-start = (f32[144,128]{1,0:T(8,128)}, f32[144,128]{1,0:T(8,128)S(1)}, u32[]{:S(2)}, u32[]{:S(2)}) collective-permute-start(f32[144,128]{1,0:T(8,128)} %get-tuple-element.15), channel_id=1, source_target_pairs={{0,4},{4,0},{8,12},{12,8},{16,20},{20,16},{24,28},{28,24},{1,5},{5... | collective-permute-start | bytes 221192 | tf_op jit(solution)/shard_map/ppermute | solution.py:336
  5.5 6.1 %collective-permute-start.1 = (f32[144,128]{1,0:T(8,128)}, f32[144,128]{1,0:T(8,128)S(1)}, u32[]{:S(2)}, u32[]{:S(2)}) collective-permute-start(f32[144,128]{1,0:T(8,128)} %get-tuple-element.16), channel_id=1, source_target_pairs={{4,8},{8,4},{12,16},{16,12},{20,24},{24,20},{28,0},{0,28},{5,9},{9... | collective-permute-start | bytes 221192 | tf_op jit(solution)/shard_map/ppermute | solution.py:336
  8.8 2.8 %copy-start = (f32[144,128]{1,0:T(8,128)}, f32[144,128]{1,0:T(8,128)S(1)}, u32[]{:S(2)}) copy-start(f32[144,128]{1,0:T(8,128)S(1)} %collective-permute-done.refs_1_.refs_4_) | copy-start | bytes 221188
  11.6 0.6 %copy-start.1 = (f32[144,128]{1,0:T(8,128)}, f32[144,128]{1,0:T(8,128)S(1)}, u32[]{:S(2)}) copy-start(f32[144,128]{1,0:T(8,128)S(1)} %collective-permute-done.1.refs_2_.refs_5_) | copy-start | bytes 221188
  12.2 6.8 %copy-start.7 = (f32[112,128]{1,0:T(8,128)S(1)}, f32[112,128]{1,0:T(8,128)}, u32[]{:S(2)}) copy-start(f32[112,128]{1,0:T(8,128)} %get-tuple-element.17) | copy-start | bytes 172036
  12.2 6.9 %copy-start.6 = (f32[112,128]{1,0:T(8,128)S(1)}, f32[112,128]{1,0:T(8,128)}, u32[]{:S(2)}) copy-start(f32[112,128]{1,0:T(8,128)} %get-tuple-element.18) | copy-start | bytes 172036
  13.9 11.2 %collective-permute-start.4 = (f32[24,1024]{1,0:T(8,128)}, f32[24,1024]{1,0:T(8,128)S(1)}, u32[]{:S(2)}, u32[]{:S(2)}) collective-permute-start(f32[24,1024]{1,0:T(8,128)} %get-tuple-element.21), channel_id=1, source_target_pairs={{0,1},{1,0},{2,3},{3,2},{4,5},{5,4},{6,7},{7,6},{8,9},{9,8},{10,11... | collective-permute-start | bytes 294920 | tf_op jit(solution)/shard_map/ppermute | solution.py:336
  16.0 9.1 %collective-permute-start.5 = (f32[24,1024]{1,0:T(8,128)}, f32[24,1024]{1,0:T(8,128)S(1)}, u32[]{:S(2)}, u32[]{:S(2)}) collective-permute-start(f32[24,1024]{1,0:T(8,128)} %get-tuple-element.22), channel_id=1, source_target_pairs={{1,2},{2,1},{5,6},{6,5},{9,10},{10,9},{13,14},{14,13},{17,18},{18,... | collective-permute-start | bytes 294920 | tf_op jit(solution)/shard_map/ppermute | solution.py:336
  19.1 4.9 %collective-permute-start.2 = (f32[112,128]{1,0:T(8,128)S(1)}, f32[112,128]{1,0:T(8,128)S(1)}, u32[]{:S(2)}, u32[]{:S(2)}) collective-permute-start(f32[112,128]{1,0:T(8,128)S(1)} %copy-done.7), channel_id=1, source_target_pairs={{0,8},{4,12},{8,16},{12,20},{16,24},{20,28},{24,0},{28,4},{1,9},{5... | collective-permute-start | bytes 172040 | tf_op jit(solution)/shard_map/ppermute | solution.py:327
  19.1 6.0 %collective-permute-start.3 = (f32[112,128]{1,0:T(8,128)S(1)}, f32[112,128]{1,0:T(8,128)S(1)}, u32[]{:S(2)}, u32[]{:S(2)}) collective-permute-start(f32[112,128]{1,0:T(8,128)S(1)} %copy-done.6), channel_id=1, source_target_pairs={{0,12},{4,16},{8,20},{12,24},{16,28},{20,0},{24,4},{28,8},{1,13},{... | collective-permute-start | bytes 172040 | tf_op jit(solution)/shard_map/ppermute | solution.py:327
  23.9 1.3 %copy-start.4 = (f32[112,128]{1,0:T(8,128)}, f32[112,128]{1,0:T(8,128)S(1)}, u32[]{:S(2)}) copy-start(f32[112,128]{1,0:T(8,128)S(1)} %collective-permute-done.2.refs_6_) | copy-start | bytes 172036
  25.2 0.6 %copy-start.5 = (f32[112,128]{1,0:T(8,128)}, f32[112,128]{1,0:T(8,128)S(1)}, u32[]{:S(2)}) copy-start(f32[112,128]{1,0:T(8,128)S(1)} %collective-permute-done.3.refs_7_) | copy-start | bytes 172036
  25.2 0.7 %copy-start.2 = (f32[24,1024]{1,0:T(8,128)}, f32[24,1024]{1,0:T(8,128)S(1)}, u32[]{:S(2)}) copy-start(f32[24,1024]{1,0:T(8,128)S(1)} %collective-permute-done.4.refs_8_) | copy-start | bytes 294916
  25.2 0.7 %copy-start.3 = (f32[24,1024]{1,0:T(8,128)}, f32[24,1024]{1,0:T(8,128)S(1)}, u32[]{:S(2)}) copy-start(f32[24,1024]{1,0:T(8,128)S(1)} %collective-permute-done.5.refs_9_) | copy-start | bytes 294916
